TPU v7x, 768 devices: a whole 4x8x12 slice. The times are simulated.
768 devices in a mesh: wave: 64 (over y, x, core), lev: 12 (over z).
Axes of the slice: x: 4, y: 8, z: 12, core: 2. Of those that a mesh axis runs over, the one named last changes fastest.
Arguments:
- spec: bfloat16 [128, 384, 640], P('wave', 'lev'), may hold values from -0.5 to 0.5
- legendre: bfloat16 [128, 1280, 640], P('wave'), may hold values from -0.25 to 0.25
- layer_depth_share: float32 [48], P('lev'), may hold values from 0.5 to 2
- quad_weight: float32 [1280], replicated, may hold values from 8 to 32
- wave_of_slot: int32 [128], P('wave'), may hold values from 0 to 639, as said below
Outputs:
- tendency: bfloat16 [128, 384, 640], P('wave', 'lev')
Inputs may be any that keep to these rules, and one draw needn't show every extreme that they name: `wave_of_slot`: slots 2 i and 2 i + 1 hold wavenumbers m and 639 - m; no wavenumber appears twice.
All inputs are finite; a program needn't handle non-finite values.
Results may differ from a plain program's by a relative error of at most 0.0047.
The roundings to bfloat16 on the way count: a program that leaves them out, or rounds other values in their place, can miss the bound.
Values may be sent and summed in bfloat16 or wider, within the bound.
A program may use at most 128 MiB of HBM per device.

v0:
```python
import math

import jax
import jax.numpy as jnp
from jax import lax
from jax.sharding import PartitionSpec as P

full_turn = 2.0 * math.pi


def sent_to_all(x, axis):
    length = lax.axis_size(axis)
    return lax.all_to_all(jnp.broadcast_to(x[None], (length, *x.shape)), axis, 0, 0, tiled=True)


def laid_out(blocks, dim):
    dims = list(blocks.shape[1:])
    dims[dim] *= blocks.shape[0]
    return jnp.moveaxis(blocks, 0, dim).reshape(dims)


def collect(x, axis, dim):
    blocks = sent_to_all(x, axis)
    return laid_out(blocks, dim)


def carried_in(part, axis, combine, identity):
    count = lax.axis_size(axis)
    place = lax.axis_index(axis)
    ahead = count - 1 - place
    gathered = lax.all_gather(part, axis)
    state = jnp.zeros_like(part) + jnp.asarray(identity, part.dtype)

    def one(hop, state):
        source = count - 1 - hop
        return combine(state, lax.dynamic_index_in_dim(gathered, source, 0, False))

    return lax.fori_loop(0, ahead, one, state)


def rate_bundle(
    eastward_velocity,
    northward_velocity,
    local_curl_spin,
    thermal_state,
    planetary_rotation_effect,
    processor_dimension,
):
    absolute = local_curl_spin + planetary_rotation_effect
    return jnp.stack(
        [
            absolute * eastward_velocity,
            absolute * northward_velocity,
            0.5 * (eastward_velocity * eastward_velocity + northward_velocity * northward_velocity),
            eastward_velocity * thermal_state,
        ],
        axis=processor_dimension,
    )


def row_latitudes(device, per_dev, total_lat):
    row_ids = jnp.arange(per_dev, dtype=jnp.int32)
    quarter = per_dev // 4
    block_ids = row_ids // 4
    hemisphere = row_ids // 2 % 2
    member = row_ids % 2
    first_dist = device * quarter + block_ids
    pole_dist = jnp.where(member == 0, first_dist, total_lat // 2 - 1 - first_dist)
    return jnp.where(hemisphere == 0, pole_dist, total_lat - 1 - pole_dist)


def add_terms(earlier, later):
    return earlier + later


def body(spec, legendre, layer_depth_share, quad_weight, wave_of_slot):
    number_of_slots, columns, degree_list = spec.shape
    total_lat = legendre.shape[1]
    groups = lax.axis_size("wave")
    device = lax.axis_index("wave")
    per_dev = total_lat // groups
    layers_on_processor = layer_depth_share.shape[0]
    field_stack = columns // (2 * layers_on_processor)
    flat_rows = field_stack * layers_on_processor
    max_points = 20 + 4 * (total_lat // 2 - 1)
    all_waves = collect(wave_of_slot, "wave", 0)
    wave_count = all_waves.shape[0]
    weight_two = jnp.where(all_waves == 0, 1.0, 2.0).astype(jnp.float32)
    degree_index = jnp.arange(degree_list, dtype=jnp.int32)
    valid_cols = degree_index[None, :] < (degree_list - wave_of_slot)[:, None]
    screened_entries = jnp.where(valid_cols[:, None, :], spec, jnp.zeros_like(spec))
    thermal_state = screened_entries.reshape(
        number_of_slots, 2, field_stack, layers_on_processor, degree_list
    )[:, :, 3].astype(jnp.float32)
    scaled_entries = thermal_state * layer_depth_share[None, None, :, None]
    below_sum = jnp.flip(jnp.cumsum(jnp.flip(scaled_entries, 2), 2), 2)
    deeper = carried_in(
        below_sum[:, :, 0],
        "lev",
        add_terms,
        jnp.zeros((number_of_slots, 2, degree_list), jnp.float32),
    )
    geopot = below_sum + deeper[:, :, None, :]
    fourier = jnp.einsum(
        "sln,scn->lsc", legendre, screened_entries, preferred_element_type=jnp.float32
    ).astype(jnp.bfloat16)
    send_order = row_latitudes(
        jnp.arange(groups, dtype=jnp.int32)[:, None], per_dev, total_lat
    ).reshape(-1)
    send_rows = jnp.take(fourier, send_order, axis=0).reshape(total_lat, number_of_slots * columns)
    received = lax.all_to_all(send_rows, "wave", split_axis=0, concat_axis=1, tiled=True)
    coeffs = received.reshape(per_dev, wave_count, 2, flat_rows)
    latitudes = row_latitudes(device, per_dev, total_lat)
    lengths = 20 + 4 * jnp.minimum(latitudes, total_lat - 1 - latitudes)
    planetary_rotation_effect = 2.0 * jnp.cos(
        (latitudes.astype(jnp.float32) + 0.5) * (math.pi / total_lat)
    )
    row_scale = quad_weight[latitudes] / lengths.astype(jnp.float32)
    quarter = per_dev // 4
    pair_points = max_points + 20
    tile_count = -(-pair_points // 128)
    padded = tile_count * 128
    pair_len = lengths.reshape(quarter, 2, 2)[:, 0, :]
    first_len = pair_len[:, 0:1]
    second_len = pair_len[:, 1:2]
    points = jnp.arange(padded, dtype=jnp.int32)[None, :]
    first_lat = points < first_len
    in_pair = points < pair_points
    local_idx = jnp.where(first_lat, points, points - first_len)
    point_len = jnp.where(first_lat, first_len, second_len)
    phase_int = all_waves[None, :, None] * local_idx[:, None, :] % point_len[:, None, :]
    angles = phase_int.astype(jnp.float32) * full_turn / point_len.astype(jnp.float32)[:, None, :]
    cosine = jnp.cos(angles)
    sine_vals = jnp.sin(angles)
    resolved = (2 * all_waves[None, :, None] < point_len[:, None, :]) & in_pair[:, None, :]
    amplitude = jnp.where(resolved, weight_two[None, :, None], 0.0)
    forward_tab = jnp.concatenate([amplitude * cosine, -(amplitude * sine_vals)], 1).astype(
        jnp.bfloat16
    )
    back_tab = jnp.concatenate(
        [jnp.where(resolved, cosine, 0.0), -jnp.where(resolved, sine_vals, 0.0)], 1
    ).astype(jnp.bfloat16)
    forward_tiles = forward_tab.reshape(quarter, 2 * wave_count, tile_count, 128)
    back_tiles = back_tab.reshape(quarter, 2 * wave_count, tile_count, 128)
    tile_start = jnp.arange(tile_count, dtype=jnp.int32)[None, :] * 128
    owner_second = tile_start + 128 > first_len
    boundary = first_len[:, 0] // 128
    is_bound = jnp.arange(tile_count, dtype=jnp.int32)[None, :] == boundary[:, None]
    first_tiles = first_lat.reshape(quarter, tile_count, 128)
    stacked = coeffs.reshape(quarter, 2, 2, wave_count, 2, flat_rows).transpose(0, 1, 2, 4, 3, 5)
    stacked = stacked.reshape(quarter, 2, 2, 2 * wave_count, flat_rows)
    coef_tiles = jnp.where(
        owner_second[:, None, :, None, None],
        stacked[:, :, 1][:, :, None],
        stacked[:, :, 0][:, :, None],
    )
    grid_tiles = jnp.einsum(
        "qatkf,qktp->qaftp", coef_tiles, forward_tiles, preferred_element_type=jnp.float32
    )
    bound_fwd = jnp.take_along_axis(forward_tiles, boundary[:, None, None, None], axis=2)[:, :, 0]
    bound_back = jnp.take_along_axis(back_tiles, boundary[:, None, None, None], axis=2)[:, :, 0]
    edge_grid = jnp.einsum(
        "qakf,qkp->qafp", stacked[:, :, 0], bound_fwd, preferred_element_type=jnp.float32
    )
    use_edge = is_bound[:, :, None] & first_tiles
    grid_tiles = jnp.where(use_edge[:, None, None], edge_grid[:, :, :, None, :], grid_tiles)
    grid_vals = grid_tiles.reshape(quarter, 2, field_stack, layers_on_processor, padded)
    row_cor = planetary_rotation_effect.reshape(quarter, 2, 2)
    point_cor = jnp.where(first_lat[:, None, :], row_cor[:, :, 0:1], row_cor[:, :, 1:2])[
        :, :, None, :
    ]
    products = rate_bundle(
        grid_vals[:, :, 0], grid_vals[:, :, 1], grid_vals[:, :, 2], grid_vals[:, :, 3], point_cor, 2
    )
    products = products.astype(jnp.bfloat16).reshape(quarter, 2, flat_rows, tile_count, 128)
    keep = jnp.where(owner_second[:, :, None], jnp.logical_not(first_tiles), first_tiles)
    main_prods = jnp.where(keep[:, None, None], products, jnp.zeros_like(products))
    per_tile = jnp.einsum(
        "qaftp,qktp->qatkf", main_prods, back_tiles, preferred_element_type=jnp.float32
    )
    bound_prods = jnp.take_along_axis(products, boundary[:, None, None, None, None], axis=3)[
        :, :, :, 0
    ]
    bound_first = jnp.take_along_axis(first_tiles, boundary[:, None, None], axis=1)[:, 0]
    bound_prods = jnp.where(bound_first[:, None, None, :], bound_prods, jnp.zeros_like(bound_prods))
    edge_back = jnp.einsum(
        "qafp,qkp->qakf", bound_prods, bound_back, preferred_element_type=jnp.float32
    )
    owner_mask = owner_second[:, None, :, None, None]
    first_ret = jnp.sum(jnp.where(owner_mask, 0.0, per_tile), axis=2) + edge_back
    second_ret = jnp.sum(jnp.where(owner_mask, per_tile, 0.0), axis=2)
    returned = jnp.stack([first_ret, second_ret], axis=2)
    returned = (returned * row_scale.reshape(quarter, 2, 2)[:, :, :, None, None]).astype(
        jnp.bfloat16
    )
    out_rows = returned.reshape(quarter, 2, 2, 2, wave_count, flat_rows).transpose(0, 1, 2, 4, 3, 5)
    out_rows = out_rows.reshape(per_dev, wave_count * columns)
    gathered_rows = lax.all_to_all(out_rows, "wave", split_axis=1, concat_axis=0, tiled=True)
    inverse = (
        jnp.zeros((total_lat,), jnp.int32)
        .at[send_order]
        .set(jnp.arange(total_lat, dtype=jnp.int32))
    )
    back_fourier = jnp.take(gathered_rows, inverse, axis=0).reshape(
        total_lat, number_of_slots, columns
    )
    tendency = jnp.einsum(
        "lsc,sln->scn", back_fourier, legendre, preferred_element_type=jnp.float32
    )
    tendency = tendency.reshape(number_of_slots, 2, field_stack, layers_on_processor, degree_list)
    tendency = tendency.at[:, :, 2].add(geopot)
    tendency = jnp.where(valid_cols[:, None, None, None, :], tendency, 0.0)
    return tendency.reshape(number_of_slots, columns, degree_list).astype(jnp.bfloat16)


def solution(mesh):
    in_specs = (P("wave", "lev", None), P("wave", None, None), P("lev"), P(), P("wave"))
    out_specs = P("wave", "lev", None)
    return jax.shard_map(body, mesh=mesh, in_specs=in_specs, out_specs=out_specs, check_vma=False)
```

profile of v0, /device:TPU:1, one launch (start us, length us, event | category | flops | bytes accessed | tf_op | source)
XLA Modules:
  0.0 325.4 jit_solution(463046913006369650)
XLA Ops:
  0.0 1.4 broadcast_in_dim.311
  1.4 15.2 %all-to-all-start = ((s32[64,1,2]{2,1,0:T(1,128)}), s32[64,1,2]{2,1,0:T(1,128)}, u32[]{:S(2)}, u32[]{:S(2)}) async-start(s32[64,1,2]{2,1,0:T(1,128)} %broadcast_in_dim.311), calls=%async_computation | async-start | bytes 65536 | tf_op jit(solution)/shard_map/all_to_all | solution.py:13
  24.8 1.2 copy.63
  26.1 4.6 %gather_fusion = bf16[1280,2,32]{2,1,0:T(2,128)(2,1)} fusion(bf16[1280,2,32]{2,1,0:T(2,128)(2,1)} %copy.63, s32[2048]{0:T(1024)} %pad_clamp_fusion.1), kind=kCustom, calls=%fused_computation.2 | custom fusion | bytes 332800 | tf_op jit(solution)/shard_map/jit(_take)/gather | solution.py:110
  30.7 2.2 gather.33
  36.7 5.4 %scatter_custom_fusion = s32[1280]{0:T(1024)S(1)} fusion(s32[1280]{0:T(1024)} %copy-done.12, s32[1280]{0:T(1024)S(1)} %iota.344, s32[]{:T(128)} %constant.324.clone.1), kind=kCustom, calls=%fused_computation.131 | custom fusion | bytes 5632 | tf_op jit(solution)/shard_map/scatter | solution.py:202
  44.1 24.0 %all-gather = f32[24,2,1,640]{3,1,2,0:T(2,128)S(1)} all-gather(f32[2,2,1,640]{3,1,2,0:T(2,128)S(1)} %copy.79), channel_id=2, replica_groups=mesh['wave'=64,'lev'=12] {'lev'}, dimensions={0}, use_global_device_ids=true | all-gather | bytes 133120 | tf_op jit(solution)/shard_map/all_gather | solution.py:31
  69.3 1.4 compare_select_fusion
  70.7 1.4 broadcast_compare_fusion.1
  72.8 2.0 broadcast_select_fusion.1
  75.5 1.3 broadcast_select_fusion.4
  78.1 1.9 reshape.1297
  80.1 1.4 copy.73
  82.1 15.8 %all-to-all-start.1 = ((bf16[64,2,640]{2,1,0:T(2,128)(2,1)}), bf16[64,2,640]{2,1,0:T(2,128)(2,1)S(1)}, u32[]{:S(2)}, u32[]{:S(2)}) async-start(bf16[64,2,640]{2,1,0:T(2,128)(2,1)} %reshape.1297), calls=%async_computation.1 | async-start | bytes 327680 | tf_op jit(solution)/shard_map/all_to_all | solution.py:111
  98.5 2.1 reduce.9
  100.5 1.4 broadcast_in_dim_reshape.2
  103.2 109.6 %fusion = (bf16[5,128,21,128]{3,1,2,0:T(8,128)(2,1)S(1)}, bf16[5,128,21,128]{3,1,2,0:T(8,128)(2,1)}, bf16[5,128,21,128]{3,1,2,0:T(8,128)(2,1)}, bf16[5,128,21,128]{3,1,2,0:T(8,128)(2,1)}) fusion(f32[128]{0:T(128)S(1)} %compare_select_fusion.20, s32[5,21,128]{2,1,0:T(8,128)} %get-tuple-element.99, s32[128]{0:T(128)S(1)} %broadcast_multiply_fusion, ...), kind=kLoop, calls=%fused_computation.12 | loop fusion | flops 41287680 | bytes 13995264 | tf_op jit(solution)/shard_map/convert.5
  212.8 6.7 %pad_maximum_fusion.1 = bf16[5,256,21,128]{3,1,2,0:T(8,128)(2,1)} fusion(bf16[5,128,21,128]{3,1,2,0:T(8,128)(2,1)} %get-tuple-element.92, bf16[5,128,21,128]{3,1,2,0:T(8,128)(2,1)S(1)} %get-tuple-element.91), kind=kLoop, calls=%fused_computation.19 | loop fusion | flops 13762560 | bytes 13762560 | tf_op jit(solution)/shard_map/concatenate | solution.py:137
  219.5 4.3 %gather_fusion.5 = bf16[5,256,128]{2,1,0:T(8,128)(2,1)} fusion(bf16[5,256,21,128]{3,1,2,0:T(8,128)(2,1)} %pad_maximum_fusion.1, s32[5]{0:T(128)S(1)} %get-tuple-element.117), kind=kCustom, calls=%fused_computation.clone | custom fusion | bytes 655400 | tf_op jit(solution)/shard_map/jit(take_along_axis)/gather | solution.py:160
  223.8 6.8 %pad_maximum_fusion = bf16[5,256,21,128]{3,1,2,0:T(8,128)(2,1)} fusion(bf16[5,128,21,128]{3,1,2,0:T(8,128)(2,1)} %get-tuple-element.94, bf16[5,128,21,128]{3,1,2,0:T(8,128)(2,1)} %get-tuple-element.93), kind=kLoop, calls=%fused_computation.18 | loop fusion | flops 13762560 | bytes 13762560 | tf_op jit(solution)/shard_map/concatenate | solution.py:140
  230.6 4.3 %gather_fusion.6 = bf16[5,256,128]{2,1,0:T(8,128)(2,1)} fusion(bf16[5,256,21,128]{3,1,2,0:T(8,128)(2,1)} %pad_maximum_fusion, s32[5]{0:T(128)S(1)} %get-tuple-element.117), kind=kCustom, calls=%fused_computation.1.clone | custom fusion | bytes 655400 | tf_op jit(solution)/shard_map/jit(take_along_axis)/gather | solution.py:161
  235.9 1.8 copy.64
  237.7 4.2 %reshape_reshape.3 = bf16[5,2,2,128,2,16]{5,4,3,2,1,0:T(2,128)(2,1)} reshape(bf16[20,64,64]{2,1,0:T(8,128)(2,1)} %copy.64) | data formatting | bytes 327680 | tf_op jit(solution)/shard_map/reshape;reshape | solution.py:150
  241.9 3.6 %copy.65 = bf16[5,2,2,2,128,16]{4,3,5,1,0,2:T(2,128)(2,1)} copy(bf16[5,2,2,2,128,16]{5,3,4,2,1,0:T(2,128)(2,1)} %bitcast.137) | data formatting | bytes 327680 | tf_op jit(solution)/shard_map/transpose | solution.py:150
  246.6 1.2 fusion.27
  247.8 3.8 %bitcast_select_fusion = f32[5,2,16,21,128]{4,2,1,3,0:T(8,128)S(1)} fusion(pred[5,21]{1,0:T(8,128)(4,1)} %copy-done.16, bf16[5,2,256,16]{2,3,1,0:T(8,128)(2,1)S(1)} %get-tuple-element.96, bf16[5,2,256,16]{2,3,1,0:T(8,128)(2,1)S(1)} %get-tuple-element.95, f32[5,2,16,128]{3,2,1,0:T(8,128)S(1)} %fusion.27, pred[5,21,128]{2,1,0:T(8,128)(4,1)} %get-tuple-element.101, ...), kind=kOutput, calls=%fused_computation.36 | convolution fusion | flops 235253760 | bytes 8860905 | tf_op jit(solution)/shard_map/qatkf,qktp->qaftp/dot_general | solution.py:157
  251.7 2.3 copy.66
  254.0 2.8 reshape.1194
  256.8 1.8 multiply_convert_fusion.2
  258.5 1.6 pad_maximum_fusion.2
  260.1 2.4 convert_element_type.62
  262.6 2.2 copy.72
  264.8 1.3 broadcast_select_fusion
  266.3 4.8 %fusion.64 = f32[5,21,256,32]{2,3,1,0:S(1)} fusion(bf16[5,21,128,32]{2,3,1,0:T(8,128)(2,1)S(1)} %bitcast.141, bf16[5,128,21,128]{3,1,2,0:T(8,128)(2,1)} %get-tuple-element.94, bf16[5,128,21,128]{3,1,2,0:T(8,128)(2,1)} %get-tuple-element.93), kind=kOutput, calls=%fused_computation.203 | convolution fusion | flops 233963520 | bytes 11182080
  271.1 1.3 select_reduce_fusion.1
  272.4 1.7 gather_fusion.4
  274.2 2.0 fusion.21
  276.1 1.7 stack.18
  279.8 2.2 copy.74
  281.9 4.2 %all_to_all.31 = bf16[20,64,64]{2,1,0:T(8,128)(2,1)} reshape(bf16[5,2,2,128,2,16]{5,4,3,2,1,0:T(2,128)(2,1)} %copy.74) | data formatting | bytes 327680 | tf_op jit(solution)/shard_map/all_to_all | solution.py:198
  286.1 1.9 copy.89
  288.1 1.9 reshape.1299
  290.0 10.3 %all-to-all-start.2 = ((bf16[64,2,640]{2,1,0:T(2,128)(2,1)}), bf16[64,2,640]{2,1,0:T(2,128)(2,1)S(1)}, u32[]{:S(2)}, u32[]{:S(2)}) async-start(bf16[64,2,640]{2,1,0:T(2,128)(2,1)} %reshape.1299), calls=%async_computation.2 | async-start | bytes 327680 | tf_op jit(solution)/shard_map/all_to_all | solution.py:198
  300.4 11.6 %all-to-all-done.2 = bf16[64,2,640]{2,1,0:T(2,128)(2,1)S(1)} async-done(((bf16[64,2,640]{2,1,0:T(2,128)(2,1)}), bf16[64,2,640]{2,1,0:T(2,128)(2,1)S(1)}, u32[]{:S(2)}, u32[]{:S(2)}) %all-to-all-start.2) | async-done | bytes 163872 | tf_op jit(solution)/shard_map/all_to_all | solution.py:198
  313.0 1.8 bitcast_bitcast_fusion
  314.8 1.8 all_to_all.34
  316.6 4.2 %gather_fusion.2 = bf16[1280,64]{1,0:T(8,128)(2,1)} fusion(bf16[1280,64]{1,0:T(8,128)(2,1)} %all_to_all.34, s32[2048]{0:T(1024)S(1)} %pad_clamp_fusion), kind=kCustom, calls=%fused_computation.4 | custom fusion | bytes 332800 | tf_op jit(solution)/shard_map/jit(_take)/gather | solution.py:204
  321.9 1.3 fusion.33
  (129 shorter events, 28.5 us)
Async XLA Ops:
  0.0 23.8 %copy-start = (bf16[2,1280,640]{2,1,0:T(8,128)(2,1)S(1)}, bf16[2,1280,640]{2,1,0:T(8,128)(2,1)}, u32[]{:S(2)}) copy-start(bf16[2,1280,640]{2,1,0:T(8,128)(2,1)} %param.12) | copy-start | bytes 9830404
  0.0 33.6 %copy-start.1 = (f32[1280]{0:T(1024)S(1)}, f32[1280]{0:T(1024)}, u32[]{:S(2)}) copy-start(f32[1280]{0:T(1024)} %param.14) | copy-start | bytes 15364
  1.4 80.7 %all-to-all-start = ((s32[64,1,2]{2,1,0:T(1,128)}), s32[64,1,2]{2,1,0:T(1,128)}, u32[]{:S(2)}, u32[]{:S(2)}) async-start(s32[64,1,2]{2,1,0:T(1,128)} %broadcast_in_dim.311), calls=%async_computation | async-start | bytes 65536 | tf_op jit(solution)/shard_map/all_to_all | solution.py:13
  22.1 1.6 copy-start.12
  22.8 0.9 copy-start.14
  42.1 33.4 %copy-start.7 = (s32[1280]{0:T(1024)}, s32[1280]{0:T(1024)S(1)}, u32[]{:S(2)}) copy-start(s32[1280]{0:T(1024)S(1)} %scatter_custom_fusion) | copy-start | bytes 15364
  43.5 0.6 copy-start.3
  69.3 6.2 %copy-start.16 = (pred[5,21]{1,0:T(8,128)(4,1)}, pred[5,21]{1,0:T(8,128)(4,1)S(1)}, u32[]{:S(2)}) copy-start(pred[5,21]{1,0:T(8,128)(4,1)S(1)} %get-tuple-element.116) | copy-start | bytes 319
  72.8 9.3 %copy-start.5 = (s32[5]{0:T(128)}, s32[5]{0:T(128)S(1)}, u32[]{:S(2)}) copy-start(s32[5]{0:T(128)S(1)} %get-tuple-element.118) | copy-start | bytes 64
  82.1 152.8 %all-to-all-start.1 = ((bf16[64,2,640]{2,1,0:T(2,128)(2,1)}), bf16[64,2,640]{2,1,0:T(2,128)(2,1)S(1)}, u32[]{:S(2)}, u32[]{:S(2)}) async-start(bf16[64,2,640]{2,1,0:T(2,128)(2,1)} %reshape.1297), calls=%async_computation.1 | async-start | bytes 327680 | tf_op jit(solution)/shard_map/all_to_all | solution.py:111
  212.8 6.8 %copy-start.2 = (bf16[5,128,21,128]{3,1,2,0:T(8,128)(2,1)}, bf16[5,128,21,128]{3,1,2,0:T(8,128)(2,1)S(1)}, u32[]{:S(2)}) copy-start(bf16[5,128,21,128]{3,1,2,0:T(8,128)(2,1)S(1)} %get-tuple-element.91) | copy-start | bytes 10321924
  251.7 13.2 %copy-start.9 = (pred[5,21,128]{2,1,0:T(8,128)(4,1)S(1)}, pred[5,21,128]{2,1,0:T(8,128)(4,1)}, u32[]{:S(2)}) copy-start(pred[5,21,128]{2,1,0:T(8,128)(4,1)} %get-tuple-element.102) | copy-start | bytes 40324
  266.2 4.8 %copy-start.17 = (pred[5,21]{1,0:T(8,128)(4,1)S(1)}, pred[5,21]{1,0:T(8,128)(4,1)}, u32[]{:S(2)}) copy-start(pred[5,21]{1,0:T(8,128)(4,1)} %copy-done.16) | copy-start | bytes 319
  266.3 6.1 %copy-start.6 = (s32[5]{0:T(128)S(1)}, s32[5]{0:T(128)}, u32[]{:S(2)}) copy-start(s32[5]{0:T(128)} %copy-done.5) | copy-start | bytes 64
  266.3 7.9 %copy-start.18 = (pred[5,128]{1,0:T(8,128)(4,1)S(1)}, pred[5,128]{1,0:T(8,128)(4,1)}, u32[]{:S(2)}) copy-start(pred[5,128]{1,0:T(8,128)(4,1)} %broadcast_select_fusion.4) | copy-start | bytes 1924
  266.3 7.9 %copy-start.19 = (pred[5]{0:T(512)(128)(4,1)S(1)}, pred[5]{0:T(512)(128)(4,1)}, u32[]{:S(2)}) copy-start(pred[5]{0:T(512)(128)(4,1)} %get-tuple-element.85) | copy-start | bytes 19
  266.3 7.9 %copy-start.20 = (pred[5]{0:T(512)(128)(4,1)S(1)}, pred[5]{0:T(512)(128)(4,1)}, u32[]{:S(2)}) copy-start(pred[5]{0:T(512)(128)(4,1)} %and_bitcast_fusion) | copy-start | bytes 19
  266.3 12.2 %copy-start.11 = (f32[5,2,2]{1,0,2:T(8,128)S(1)}, f32[5,2,2]{1,0,2:T(8,128)}, u32[]{:S(2)}) copy-start(f32[5,2,2]{1,0,2:T(8,128)} %copy.73) | copy-start | bytes 244
  271.1 29.2 %copy-start.13 = (s32[1280]{0:T(1024)S(1)}, s32[1280]{0:T(1024)}, u32[]{:S(2)}) copy-start(s32[1280]{0:T(1024)} %compare_select_fusion.5) | copy-start | bytes 15364
  271.1 29.3 %copy-start.8 = (s32[1280]{0:T(1024)S(1)}, s32[1280]{0:T(1024)}, u32[]{:S(2)}) copy-start(s32[1280]{0:T(1024)} %copy-done.7) | copy-start | bytes 15364
  279.7 44.4 %copy-start.4 = (f32[2,2,4,640]{3,0,2,1:T(2,128)S(1)}, f32[2,2,4,640]{3,0,2,1:T(2,128)}, u32[]{:S(2)}) copy-start(f32[2,2,4,640]{3,0,2,1:T(2,128)} %copy-done.3) | copy-start | bytes 122884
  279.7 44.4 %copy-start.10 = (f32[2,2,640]{2,0,1:T(2,128)S(1)}, f32[2,2,640]{2,0,1:T(2,128)}, u32[]{:S(2)}) copy-start(f32[2,2,640]{2,0,1:T(2,128)} %copy.80) | copy-start | bytes 30724
  279.7 44.5 %copy-start.15 = (pred[2,640]{1,0:T(4,128)(4,1)S(1)}, pred[2,640]{1,0:T(4,128)(4,1)}, u32[]{:S(2)}) copy-start(pred[2,640]{1,0:T(4,128)(4,1)} %copy-done.14) | copy-start | bytes 3844
  290.0 22.0 %all-to-all-start.2 = ((bf16[64,2,640]{2,1,0:T(2,128)(2,1)}), bf16[64,2,640]{2,1,0:T(2,128)(2,1)S(1)}, u32[]{:S(2)}, u32[]{:S(2)}) async-start(bf16[64,2,640]{2,1,0:T(2,128)(2,1)} %reshape.1299), calls=%async_computation.2 | async-start | bytes 327680 | tf_op jit(solution)/shard_map/all_to_all | solution.py:198
where the time goes:
time: 328 us; the launch traced here: 325 us
  other arithmetic  151 us (46%)
  local copies, waits for them, and re-layouts  81.8 us (25%)
  starting transfers between devices  41.3 us (13%)
  blocking collectives  24 us (7%)
  matrix products  14.1 us (4%)
  waiting for transfers between devices  11.6 us (4%)
    another operation x2, other arithmetic  111 us
    all_gather x1, blocking collectives, carried_in(): gathered = lax.all_gather(part, axis)  24 us
    all_to_all x1, starting transfers between devices, body(): lax.all_to_all(send_rows, 'wave', split_axis=0, concat_axis=1, tiled=True)  15.8 us
    all_to_all x1, starting transfers between devices, sent_to_all(): lax.all_to_all(jnp.broadcast_to(x[None], (length, *x.shape)), axis, 0, 0,...  15.2 us
    all_to_all x1, waiting for transfers between devices, body(): lax.all_to_all(out_rows, 'wave', split_axis=1, concat_axis=0, tiled=True)  11.6 us
    all_to_all x1, starting transfers between devices, body(): lax.all_to_all(out_rows, 'wave', split_axis=1, concat_axis=0, tiled=True)  10.3 us
    all_to_all x4, local copies, waits for them, and re-layouts, body(): lax.all_to_all(out_rows, 'wave', split_axis=1, concat_axis=0, tiled=True)  9.75 us
    gather x2, local copies, waits for them, and re-layouts, body(): jnp.take(fourier, send_order, axis=0)  6.78 us
  transfers between devices with their start and end apart: 3, of which 1 were waited for; matrix products, arithmetic and copies ran while one was open for 54% of the time, Pallas kernels for 0%

commit v1 on v0

v1 whole, which is shorter than its diff:
```python
import functools
import math

import jax
import jax.numpy as jnp
from jax import lax
from jax.experimental import pallas as pl
from jax.experimental.pallas import tpu as pltpu
from jax.sharding import PartitionSpec as P

MESH = pl.DeviceIdType.MESH
F32 = jnp.float32
BF16 = jnp.bfloat16
ROWS = 16
LOW = 64
NT = (((1,), (1,)), ((), ()))


def round_up(x, step):
    return -(-x // step) * step


def iota(shape, dim):
    return lax.broadcasted_iota(jnp.int32, shape, dim)


def cos_sin(turns, quarter, length):
    count = jnp.floor(turns * (1.0 / quarter) + 0.5)
    x = (turns - count * quarter) * (2.0 * math.pi / length)
    y = x * x
    sine = x + x * y * (-1 / 6 + y * (1 / 120 + y * (-1 / 5040 + y * (1 / 362880))))
    cosine = 1.0 + y * (-0.5 + y * (1 / 24 + y * (-1 / 720 + y * (1 / 40320))))
    turn = count.astype(jnp.int32)
    swap = (turn & 1) == 1
    one = jnp.where(swap, sine, cosine)
    two = jnp.where(swap, cosine, sine)
    return jnp.where(((turn + 1) & 2) == 2, -one, one), jnp.where((turn & 2) == 2, -two, two)


class Plan:
    def __init__(self, mesh):
        self.groups = mesh.shape["wave"]
        self.depth = mesh.shape["lev"]
        self.lat = 1280
        self.span = 640
        self.quarter = self.lat // 4
        self.quads = self.quarter // self.groups
        self.blocks = []
        first = 0
        for quad in range(self.quads):
            low = quad * self.groups
            high = low + self.groups - 1
            for which in range(2):
                longest = 20 + 4 * (high if which == 0 else self.lat // 2 - 1 - low)
                points = round_up(longest, 128)
                self.blocks.append((quad, which, points, first))
                first += points
        self.table_rows = first
        self.coarse = round_up(max(b[2] for b in self.blocks) // LOW, 8)


def kernel(
    plan,
    spec_hbm, leg_hbm, share_hbm, quad_hbm, wave_hbm, out_ref,
    spec, leg, share, quad, waves,
    wave_row, wave_rows, stage, msg_out, msg_in, ret_out, ret_in,
    coefs, base, table, level_out, level_in, below,
    load_sem, wave_send, wave_recv, out_send, out_recv, ret_send, ret_recv, lev_send, lev_recv,
):
    n, depth, quads, span = plan.groups, plan.depth, plan.quads, plan.span
    me = lax.axis_index("wave")
    lev = lax.axis_index("lev")
    quarter = plan.quarter

    barrier = pltpu.get_barrier_semaphore()

    def greet(k, c):
        pl.semaphore_signal(barrier, inc=1, device_id={"wave": lax.rem(me + k, n)}, device_id_type=MESH)
        return c

    lax.fori_loop(1, n, greet, 0)

    def greet_level(k, c):
        pl.semaphore_signal(barrier, inc=1, device_id={"lev": k}, device_id_type=MESH)
        return c

    lax.fori_loop(lev + 1, depth, greet_level, 0)

    loads = [
        pltpu.make_async_copy(wave_hbm, waves, load_sem.at[0]),
        pltpu.make_async_copy(spec_hbm, spec, load_sem.at[1]),
        pltpu.make_async_copy(share_hbm, share, load_sem.at[2]),
        pltpu.make_async_copy(quad_hbm, quad, load_sem.at[3]),
        pltpu.make_async_copy(leg_hbm.at[0], leg.at[0], load_sem.at[4]),
        pltpu.make_async_copy(leg_hbm.at[1], leg.at[1], load_sem.at[5]),
    ]
    for load in loads:
        load.start()
    loads[0].wait()
    lane = iota((1, 128), 1)
    row = jnp.where(lane == me, waves[0], 0) + jnp.where(lane == me + n, waves[1], 0)
    wave_row[...] = row.astype(F32)
    loads[1].wait()
    loads[2].wait()

    column = iota((1, span), 1)
    masked = []
    for slot in range(2):
        live = column < span - waves[slot]
        values = jnp.where(live, spec[slot].astype(F32), 0.0)
        masked.append(values.astype(BF16))
        for part in range(2):
            total = jnp.zeros((1, span), F32)
            for l in (3, 2, 1, 0):
                at = part * 16 + 12 + l
                total = total + values[at : at + 1] * share[l]
                below[slot, part, l : l + 1, :] = total
            level_out[slot * 2 + part : slot * 2 + part + 1, :] = total

    where_row = iota((128, 32), 0)
    where_col = iota((128, 32), 1)
    column_of = (where_col // 16) * 64 + (where_col // 4 % 4) * 8 + where_col % 4
    place = []
    for k in range(4):
        which = 1 if k in (1, 2) else 0
        south = k // 2
        place.append((where_row == column_of + which * 32 + south * 4).astype(BF16))
    flip = (iota((n, n), 0) + iota((n, n), 1) == n - 1).astype(BF16)

    stage[...] = jnp.zeros_like(stage)
    for slot in range(2):
        loads[4 + slot].wait()
        sums = []
        for pair in ((0, 2), (1, 3)):
            acc = None
            for k in pair:
                weights = jnp.dot(place[k], masked[slot], preferred_element_type=F32).astype(BF16)
                term = lax.dot_general(
                    leg[slot, k * quarter : (k + 1) * quarter, :], weights, NT, preferred_element_type=F32
                )
                acc = term if acc is None else acc + term
            sums.append(acc)
        forward, backward = sums[0], sums[1].astype(BF16)
        for b in range(quads):
            other = quads - 1 - b
            turned = jnp.dot(flip, backward[other * n : (other + 1) * n], preferred_element_type=F32)
            stage[pl.ds(slot * quads + b, n, stride=ROWS), :] = forward[b * n : (b + 1) * n] + turned
    msg_out[...] = stage[...].astype(BF16).reshape(n, ROWS, 128)

    pl.semaphore_wait(barrier, n - 1 + lev)

    def send_wave(k, c):
        pltpu.make_async_remote_copy(
            wave_row, wave_rows.at[me], wave_send, wave_recv,
            device_id={"wave": lax.rem(me + k, n)}, device_id_type=MESH,
        ).start()
        return c

    lax.fori_loop(1, n, send_wave, 0)

    def send_out(k, c):
        to = lax.rem(me + k, n)
        pltpu.make_async_remote_copy(
            msg_out.at[to], msg_in.at[me], out_send, out_recv, device_id={"wave": to}, device_id_type=MESH
        ).start()
        return c

    lax.fori_loop(1, n, send_out, 0)

    def level_copy(source, to):
        return pltpu.make_async_remote_copy(
            level_out, level_in.at[source], lev_send.at[to], lev_recv.at[source],
            device_id={"lev": to}, device_id_type=MESH,
        )

    def send_level(k, c):
        level_copy(lev, k).start()
        return c

    lax.fori_loop(0, lev, send_level, 0)
    wave_rows[me] = wave_row[...]
    msg_in[me] = msg_out[me]
    others = pl.ds(0, n - 1)
    pltpu.make_async_copy(wave_rows.at[others], wave_rows.at[others], wave_recv).wait()
    m = jnp.sum(wave_rows[...], axis=0)

    loads[3].wait()
    rows = LOW + plan.coarse
    index = iota((rows, 1), 0)
    step = jnp.where(index < LOW, index, (index - LOW) * LOW).astype(F32)
    turns = step * m
    lengths = []
    for at, (b, which, points, first) in enumerate(plan.blocks):
        q = me + b * n
        if which == 1:
            q = plan.lat // 2 - 1 - q
        quart = (5 + q).astype(F32)
        lengths.append((q, quart * 4.0))
        c, s = cos_sin(turns, quart, quart * 4.0)
        base[at, 0] = c
        base[at, 1] = s

    for at, (b, which, points, first) in enumerate(plan.blocks):

        def expand(a, c, at=at, first=first):
            cl, sl = base[at, 0, pl.ds(0, LOW), :], base[at, 1, pl.ds(0, LOW), :]
            ch, sh = base[at, 0, pl.ds(LOW + a, 1), :], base[at, 1, pl.ds(LOW + a, 1), :]
            to = pl.ds(pl.multiple_of(first + a * LOW, LOW), LOW)
            table[to, 0:128] = (ch * cl - sh * sl).astype(BF16)
            table[to, 128:256] = (sh * cl + ch * sl).astype(BF16)
            return c

        lax.fori_loop(0, points // LOW, expand, 0)

    pltpu.make_async_copy(msg_in.at[others], msg_in.at[others], out_recv).wait()
    stage[...] = msg_in[...].reshape(n * ROWS, 128).astype(F32)
    double = jnp.where(m == 0.0, 1.0, 2.0)
    open_ = [2.0 * m < length for _, length in lengths]
    for b in range(quads):
        rows_in = [stage[pl.ds(slot * quads + b, n, stride=ROWS), :] for slot in range(2)]
        turned = jnp.concatenate(rows_in, axis=0).T
        for which in range(2):
            amplitude = jnp.where(open_[2 * b + which], double, 0.0)
            real = turned[which * 32 : which * 32 + 32] * amplitude
            imag = turned[64 + which * 32 : 96 + which * 32] * -amplitude
            coefs[2 * b + which] = jnp.concatenate([real, imag], axis=1).astype(BF16)

    sub = iota((8, 1), 0)
    for b in range(quads):
        sums = []
        for which in range(2):
            at = 2 * b + which
            _, _, points, first = plan.blocks[at]
            q, length = lengths[at]
            south = plan.lat - 1 - q
            lats = jnp.where(sub // 4 == 0, q, south)
            spin = 2.0 * cos_sin((2 * lats + 1).astype(F32), plan.lat * 1.0, plan.lat * 4.0)[0]
            angles = table[first : first + points, :]
            grid = lax.dot_general(coefs[at], angles, NT, preferred_element_type=F32)
            u, v, vort, temp = grid[0:8], grid[8:16], grid[16:24], grid[24:32]
            absolute = vort + spin
            inside = iota((1, points), 1).astype(F32) < length
            products = [absolute * u, absolute * v, 0.5 * (u * u + v * v), u * temp]
            products = jnp.concatenate([jnp.where(inside, p, 0.0) for p in products], axis=0).astype(BF16)
            back = jnp.dot(products, angles, preferred_element_type=F32)
            is_south = iota((32, 1), 0) // 4 % 2 == 1
            scale = jnp.where(is_south, quad[south], quad[q]) / length
            keep = open_[at]
            real = jnp.where(keep, back[:, 0:128] * scale, 0.0)
            imag = jnp.where(keep, -back[:, 128:256] * scale, 0.0)
            sums.append((real, imag))
        merged = jnp.concatenate([sums[0][0], sums[1][0], sums[0][1], sums[1][1]], axis=0).T
        for slot in range(2):
            stage[pl.ds(slot * quads + b, n, stride=ROWS), :] = merged[slot * n : (slot + 1) * n]
    ret_out[...] = stage[...].astype(BF16).reshape(n, ROWS, 128)

    def send_back(k, c):
        to = lax.rem(me + k, n)
        pltpu.make_async_remote_copy(
            ret_out.at[to], ret_in.at[me], ret_send, ret_recv, device_id={"wave": to}, device_id_type=MESH
        ).start()
        return c

    lax.fori_loop(1, n, send_back, 0)
    ret_in[me] = ret_out[me]

    def wait_level(k, acc):
        level_copy(k, lev).wait_recv()
        return acc + level_in[k]

    deeper = lax.fori_loop(lev + 1, depth, wait_level, jnp.zeros((4, span), F32))
    for slot in range(2):
        for part in range(2):
            at = slot * 2 + part
            below[slot, part] = below[slot, part] + deeper[at : at + 1]

    pltpu.make_async_copy(ret_in.at[others], ret_in.at[others], ret_recv).wait()
    stage[...] = ret_in[...].reshape(n * ROWS, 128).astype(F32)
    pick_row = iota((32, 128), 0)
    pick_col = iota((32, 128), 1)
    picked_of = (pick_row // 16) * 64 + (pick_row // 4 % 4) * 8 + pick_row % 4
    for slot in range(2):
        ahead = [stage[pl.ds(slot * quads + b, n, stride=ROWS), :].astype(BF16) for b in range(quads)]
        turned = [jnp.dot(flip, x, preferred_element_type=F32).astype(BF16) for x in ahead[::-1]]
        ahead = jnp.concatenate(ahead, axis=0)
        turned = jnp.concatenate(turned, axis=0)
        acc = jnp.zeros((32, span), F32)
        for k in range(4):
            which = 1 if k in (1, 2) else 0
            pick = (pick_col == picked_of + which * 32 + (k // 2) * 4).astype(BF16)
            left = lax.dot_general(pick, turned if k % 2 else ahead, NT, preferred_element_type=F32)
            acc = acc + jnp.dot(
                left.astype(BF16), leg[slot, k * quarter : (k + 1) * quarter, :], preferred_element_type=F32
            )
        zero = jnp.zeros((4, span), F32)
        geo = jnp.concatenate(
            [zero, zero, below[slot, 0], zero, zero, zero, below[slot, 1], zero], axis=0
        )
        live = column < span - waves[slot]
        out_ref[slot] = jnp.where(live, acc + geo, 0.0).astype(BF16)

    pltpu.make_async_copy(wave_rows.at[others], wave_rows.at[others], wave_send).wait()
    pltpu.make_async_copy(msg_out.at[others], msg_out.at[others], out_send).wait()
    pltpu.make_async_copy(ret_out.at[others], ret_out.at[others], ret_send).wait()

    def sent_level(k, c):
        level_copy(lev, k).wait_send()
        return c

    lax.fori_loop(0, lev, sent_level, 0)


def solution(mesh):
    plan = Plan(mesh)
    n, depth, span, lat = plan.groups, plan.depth, plan.span, plan.lat
    dma = pltpu.SemaphoreType.DMA

    def body(spec, legendre, layer_depth_share, quad_weight, wave_of_slot):
        any_spec = pl.BlockSpec(memory_space=pl.ANY)
        return pl.pallas_call(
            functools.partial(kernel, plan),
            out_shape=jax.ShapeDtypeStruct((2, 32, span), BF16),
            in_specs=[any_spec] * 5,
            out_specs=pl.BlockSpec(memory_space=pltpu.VMEM),
            scratch_shapes=[
                pltpu.VMEM((2, 32, span), BF16),
                pltpu.VMEM((2, lat, span), BF16),
                pltpu.SMEM((4,), F32),
                pltpu.SMEM((lat,), F32),
                pltpu.SMEM((2,), jnp.int32),
                pltpu.VMEM((1, 128), F32),
                pltpu.VMEM((n, 1, 128), F32),
                pltpu.VMEM((n * ROWS, 128), F32),
                pltpu.VMEM((n, ROWS, 128), BF16),
                pltpu.VMEM((n, ROWS, 128), BF16),
                pltpu.VMEM((n, ROWS, 128), BF16),
                pltpu.VMEM((n, ROWS, 128), BF16),
                pltpu.VMEM((2 * plan.quads, 32, 256), BF16),
                pltpu.VMEM((2 * plan.quads, 2, LOW + plan.coarse, 128), F32),
                pltpu.VMEM((plan.table_rows, 256), BF16),
                pltpu.VMEM((4, span), F32),
                pltpu.VMEM((depth, 4, span), F32),
                pltpu.VMEM((2, 2, 4, span), F32),
                dma((6,)), dma, dma, dma, dma, dma, dma, dma((depth,)), dma((depth,)),
            ],
            compiler_params=pltpu.CompilerParams(
                collective_id=0, has_side_effects=True, vmem_limit_bytes=60 * 1024 * 1024
            ),
        )(spec, legendre, layer_depth_share, quad_weight, wave_of_slot)

    in_specs = (P("wave", "lev", None), P("wave", None, None), P("lev"), P(), P("wave"))
    return jax.shard_map(body, mesh=mesh, in_specs=in_specs, out_specs=P("wave", "lev", None), check_vma=False)
```

time: 328 us -> 44.4 us (0.14)
  other arithmetic: 151 us -> 0 us
  local copies, waits for them, and re-layouts: 81.8 us -> 1.53 us
  Pallas kernels: 0 us -> 42.7 us
  starting transfers between devices: 41.3 us -> 0 us
  blocking collectives: 24 us -> 0 us
  matrix products: 14.1 us -> 0 us
  waiting for transfers between devices: 11.6 us -> 0 us
    another operation x4 -> x0, other arithmetic: 113 us -> none
    pallas_call x0 -> x1, Pallas kernels: none -> 42.7 us  [body(): pl.pallas_call(functools.partial(kernel, plan), out_shape=jax.ShapeDtypeS...]
    all_to_all x3 -> x0, starting transfers between devices: 41.3 us -> none  [the longest x1 15.8 us: body(): lax.all_to_all(send_rows, 'wave', split_axis=0, concat_axis=1, tiled=True)]
    all_gather x1 -> x0, blocking collectives: 24 us -> none  [carried_in(): gathered = lax.all_gather(part, axis)]
    gather x10 -> x0, local copies, waits for them, and re-layouts: 23.8 us -> none  [the longest x2 6.78 us: body(): jnp.take(fourier, send_order, axis=0)]
    concatenate x2 -> x0, other arithmetic: 13.5 us -> none  [the longest x1 6.75 us: body(): jnp.concatenate([jnp.where(resolved, cosine, 0.0), -jnp.where(resolved, s...]
    all_to_all x6 -> x0, local copies, waits for them, and re-layouts: 12.1 us -> none  [the longest x4 9.75 us: body(): lax.all_to_all(out_rows, 'wave', split_axis=1, concat_axis=0, tiled=True)]
    all_to_all x3 -> x0, waiting for transfers between devices: 11.6 us -> none  [the longest x1 11.6 us: body(): lax.all_to_all(out_rows, 'wave', split_axis=1, concat_axis=0, tiled=True)]
  transfers between devices with their start and end apart: 3 -> 0, of which waited for: 1 -> 0; matrix products, arithmetic and copies ran while one was open for 54% -> 0% of each run, Pallas kernels for 0% -> 0%
where the time goes in v1:
time: 44.4 us; the launch traced here: 44.2 us
  Pallas kernels  42.7 us (96%)
  local copies, waits for them, and re-layouts  1.53 us (3%)
    pallas_call x1, Pallas kernels, body(): pl.pallas_call(functools.partial(kernel, plan), out_shape=jax.ShapeDtypeS...  42.7 us
    unnamed x1, local copies, waits for them, and re-layouts  1.53 us

profile of v1, /device:TPU:1, one launch (start us, length us, event | category | flops | bytes accessed | tf_op | source)
XLA Modules:
  0.0 44.2 jit_solution(9409274929252492978)
XLA Ops:
  0.0 42.7 %shard_map.55 = bf16[2,32,640]{2,1,0:T(8,128)(2,1)} custom-call(bf16[2,32,640]{2,1,0:T(8,128)(2,1)} %spec_hbm.1, bf16[2,1280,640]{2,1,0:T(8,128)(2,1)} %leg_hbm.1, f32[4]{0:T(128)} %share_hbm.1, f32[1280]{0:T(1024)} %quad_hbm.1, s32[2]{0:T(128)} %wave_hbm.1), custom_call_target="tpu_custom_call" | custom-call | tf_op jit(solution)/shard_map/pallas_call | solution.py:320
  42.7 1.5 %copy.7 = bf16[2,32,640]{2,1,0:T(8,128)(2,1)} copy(bf16[2,32,640]{2,1,0:T(8,128)(2,1)} %shard_map.55) | data formatting | bytes 163840

commit v2 on v1

v2 whole, which is shorter than its diff:
```python
import functools
import math

import jax
import jax.numpy as jnp
from jax import lax
from jax.experimental import pallas as pl
from jax.experimental.pallas import tpu as pltpu
from jax.sharding import PartitionSpec as P

MESH = pl.DeviceIdType.MESH
F32 = jnp.float32
BF16 = jnp.bfloat16
ROWS = 16
LOW = 32
NT = (((1,), (1,)), ((), ()))


def round_up(x, step):
    return -(-x // step) * step


def iota(shape, dim):
    return lax.broadcasted_iota(jnp.int32, shape, dim)


def cos_sin(turns, quarter, length):
    count = jnp.floor(turns * (1.0 / quarter) + 0.5)
    x = (turns - count * quarter) * (2.0 * math.pi / length)
    y = x * x
    sine = x + x * y * (-1 / 6 + y * (1 / 120 + y * (-1 / 5040 + y * (1 / 362880))))
    cosine = 1.0 + y * (-0.5 + y * (1 / 24 + y * (-1 / 720 + y * (1 / 40320))))
    turn = count.astype(jnp.int32)
    swap = (turn & 1) == 1
    one = jnp.where(swap, sine, cosine)
    two = jnp.where(swap, cosine, sine)
    return jnp.where(((turn + 1) & 2) == 2, -one, one), jnp.where((turn & 2) == 2, -two, two)


class Plan:
    def __init__(self, mesh):
        self.groups = mesh.shape["wave"]
        self.depth = mesh.shape["lev"]
        self.lat = 1280
        self.span = 640
        self.quarter = self.lat // 4
        self.quads = self.quarter // self.groups
        self.blocks = []
        first = 0
        for quad in range(self.quads):
            low = quad * self.groups
            high = low + self.groups - 1
            for which in range(2):
                longest = 6 + (high if which == 0 else self.lat // 2 - 1 - low)
                points = round_up(longest, 128)
                self.blocks.append((quad, which, points, first))
                first += points
        self.table_rows = first
        self.coarse = round_up(max(b[2] for b in self.blocks) // LOW, 8)


def kernel(
    plan,
    spec_hbm, leg_hbm, share_hbm, quad_hbm, wave_hbm, out_ref,
    spec, leg, leg_turned, share, quad, waves,
    wave_row, wave_rows, stage, msg_out, msg_in, ret_out, ret_in,
    coefs, base, table, level_out, level_in, below,
    load_sem, wave_send, wave_recv, out_send, out_recv, ret_send, ret_recv, lev_send, lev_recv,
):
    n, depth, quads, span = plan.groups, plan.depth, plan.quads, plan.span
    me = lax.axis_index("wave")
    lev = lax.axis_index("lev")
    quarter = plan.quarter

    def partner(k):
        return lax.rem(me + n // 2 + (2 * (k % 2) - 1) * ((k + 1) // 2), n)

    barrier = pltpu.get_barrier_semaphore()

    def greet(k, c):
        pl.semaphore_signal(barrier, inc=1, device_id={"wave": partner(k)}, device_id_type=MESH)
        return c

    lax.fori_loop(0, n - 1, greet, 0)

    def greet_level(k, c):
        pl.semaphore_signal(barrier, inc=1, device_id={"lev": k}, device_id_type=MESH)
        return c

    lax.fori_loop(lev + 1, depth, greet_level, 0)

    loads = [
        pltpu.make_async_copy(wave_hbm, waves, load_sem.at[0]),
        pltpu.make_async_copy(spec_hbm, spec, load_sem.at[1]),
        pltpu.make_async_copy(share_hbm, share, load_sem.at[2]),
        pltpu.make_async_copy(quad_hbm, quad, load_sem.at[3]),
        pltpu.make_async_copy(leg_hbm.at[0], leg.at[0], load_sem.at[4]),
        pltpu.make_async_copy(leg_hbm.at[1], leg.at[1], load_sem.at[5]),
    ]
    for load in loads:
        load.start()
    loads[0].wait()
    lane = iota((1, 128), 1)
    row = jnp.where(lane == me, waves[0], 0) + jnp.where(lane == me + n, waves[1], 0)
    wave_row[...] = row.astype(F32)
    loads[1].wait()
    loads[2].wait()

    column = iota((1, span), 1)
    masked = []
    for slot in range(2):
        live = column < span - waves[slot]
        values = jnp.where(live, spec[slot].astype(F32), 0.0)
        masked.append(values.astype(BF16))
        for part in range(2):
            total = jnp.zeros((1, span), F32)
            for l in (3, 2, 1, 0):
                at = part * 16 + 12 + l
                total = total + values[at : at + 1] * share[l]
                below[slot, part, l : l + 1, :] = total
            level_out[slot * 2 + part : slot * 2 + part + 1, :] = total

    def which_of(k):
        return (k + 1) // 2 % 2

    where_row, where_col = iota((128, 32), 0), iota((128, 32), 1)
    column_of = (where_col // 16) * 64 + (where_col // 4 % 4) * 8 + where_col % 4
    place = [(where_row == column_of + which_of(k) * 32 + (k // 2) * 4).astype(BF16) for k in range(4)]
    flip = (iota((n, n), 0) + iota((n, n), 1) == n - 1).astype(BF16)

    def block(slot, k):
        if k % 2:
            return leg_turned[slot, k // 2]
        return leg[slot, k * quarter : (k + 1) * quarter, :]

    stage[...] = jnp.zeros_like(stage)
    for slot in range(2):
        loads[4 + slot].wait()
        for k in (1, 3):
            for b in range(quads):
                old = k * quarter + (quads - 1 - b) * n
                turned = jnp.dot(flip, leg[slot, old : old + n, :], preferred_element_type=F32)
                leg_turned[slot, k // 2, b * n : (b + 1) * n, :] = turned.astype(BF16)
        acc = None
        for k in range(4):
            weights = jnp.dot(place[k], masked[slot], preferred_element_type=F32).astype(BF16)
            term = lax.dot_general(block(slot, k), weights, NT, preferred_element_type=F32)
            acc = term if acc is None else acc + term
        for b in range(quads):
            stage[pl.ds(slot * quads + b, n, stride=ROWS), :] = acc[b * n : (b + 1) * n]
    msg_out[...] = stage[...].astype(BF16).reshape(n, ROWS, 128)

    pl.semaphore_wait(barrier, n - 1 + lev)

    def send_wave(k, c):
        pltpu.make_async_remote_copy(
            wave_row, wave_rows.at[me], wave_send, wave_recv,
            device_id={"wave": partner(k)}, device_id_type=MESH,
        ).start()
        return c

    lax.fori_loop(0, n - 1, send_wave, 0)

    def send_out(k, c):
        to = partner(k)
        pltpu.make_async_remote_copy(
            msg_out.at[to], msg_in.at[me], out_send, out_recv, device_id={"wave": to}, device_id_type=MESH
        ).start()
        return c

    lax.fori_loop(0, n - 1, send_out, 0)

    def level_copy(source, to):
        return pltpu.make_async_remote_copy(
            level_out, level_in.at[source], lev_send.at[to], lev_recv.at[source],
            device_id={"lev": to}, device_id_type=MESH,
        )

    def send_level(k, c):
        level_copy(lev, k).start()
        return c

    lax.fori_loop(0, lev, send_level, 0)
    wave_rows[me] = wave_row[...]
    msg_in[me] = msg_out[me]
    others = pl.ds(0, n - 1)
    loads[3].wait()
    pltpu.make_async_copy(wave_rows.at[others], wave_rows.at[others], wave_recv).wait()
    m = jnp.sum(wave_rows[...], axis=0)

    index = iota((LOW + plan.coarse, 1), 0)
    step = jnp.where(index < LOW, index, (index - LOW) * LOW).astype(F32)
    turns = step * m
    lengths = []
    for at, (b, which, points, first) in enumerate(plan.blocks):
        q = me + b * n
        if which == 1:
            q = plan.lat // 2 - 1 - q
        quart = (5 + q).astype(F32)
        lengths.append((q, quart, quart * 4.0))
        c, s = cos_sin(turns, quart, quart * 4.0)
        base[at, 0] = c
        base[at, 1] = s
    for at, (b, which, points, first) in enumerate(plan.blocks):
        cl, sl = base[at, 0, 0:LOW, :], base[at, 1, 0:LOW, :]
        for a in range(points // LOW):
            ch, sh = base[at, 0, LOW + a : LOW + a + 1, :], base[at, 1, LOW + a : LOW + a + 1, :]
            to = first + a * LOW
            table[to : to + LOW, 0:128] = (ch * cl - sh * sl).astype(BF16)
            table[to : to + LOW, 128:256] = (sh * cl + ch * sl).astype(BF16)

    pltpu.make_async_copy(msg_in.at[others], msg_in.at[others], out_recv).wait()
    stage[...] = msg_in[...].reshape(n * ROWS, 128).astype(F32)
    double = jnp.where(m == 0.0, 1.0, 2.0)
    parity = 1.0 - 2.0 * (m - 2.0 * jnp.floor(m * 0.5))
    keep = [2.0 * m < length for _, _, length in lengths]
    none = jnp.zeros((32, 128), F32)
    for b in range(quads):
        rows_in = [stage[pl.ds(slot * quads + b, n, stride=ROWS), :] for slot in range(2)]
        turned = jnp.concatenate(rows_in, axis=0).T
        for which in range(2):
            amplitude = jnp.where(keep[2 * b + which], double, 0.0)
            real = turned[which * 32 : which * 32 + 32] * amplitude
            imag = turned[64 + which * 32 : 96 + which * 32] * amplitude
            left = jnp.concatenate([real, none, real * parity, none], axis=0)
            right = jnp.concatenate([none, imag, none, imag * -parity], axis=0)
            coefs[2 * b + which] = jnp.concatenate([left, right], axis=1).astype(BF16)

    sub = iota((8, 1), 0)
    for b in range(quads):
        sums = []
        for which in range(2):
            at = 2 * b + which
            _, _, points, first = plan.blocks[at]
            q, quart, length = lengths[at]
            south = plan.lat - 1 - q
            lats = jnp.where(sub // 4 == 0, q, south)
            spin = 2.0 * cos_sin((2 * lats + 1).astype(F32), plan.lat * 1.0, plan.lat * 4.0)[0]
            angles = table[first : first + points, :]
            sides = lax.dot_general(coefs[at], angles, NT, preferred_element_type=F32)
            even, odd, even2, odd2 = (sides[32 * i : 32 * i + 32] for i in range(4))
            point = iota((1, points), 1).astype(F32)
            below_end = point < quart
            up_to_end = point <= quart
            later = point > 0.0
            products = []
            for grid, inside in (
                (even - odd, up_to_end),
                (even + odd, up_to_end & later),
                (even2 - odd2, below_end),
                (even2 + odd2, below_end & later),
            ):
                u, v, vort, temp = grid[0:8], grid[8:16], grid[16:24], grid[24:32]
                absolute = vort + spin
                for p in (absolute * u, absolute * v, 0.5 * (u * u + v * v), u * temp):
                    products.append(jnp.where(inside, p, 0.0))
            products = jnp.concatenate(products, axis=0).astype(BF16)
            back = jnp.dot(products, angles, preferred_element_type=F32)
            b1, b2, b3, b4 = (back[32 * i : 32 * i + 32] for i in range(4))
            real = (b1 + b2)[:, 0:128] + parity * (b3 + b4)[:, 0:128]
            imag = (b2 - b1)[:, 128:256] + parity * (b3 - b4)[:, 128:256]
            is_south = iota((32, 1), 0) // 4 % 2 == 1
            scale = jnp.where(is_south, quad[south], quad[q]) / length
            sums.append((jnp.where(keep[at], real * scale, 0.0), jnp.where(keep[at], imag * scale, 0.0)))
        merged = jnp.concatenate([sums[0][0], sums[1][0], sums[0][1], sums[1][1]], axis=0).T
        for slot in range(2):
            stage[pl.ds(slot * quads + b, n, stride=ROWS), :] = merged[slot * n : (slot + 1) * n]
    ret_out[...] = stage[...].astype(BF16).reshape(n, ROWS, 128)

    def send_back(k, c):
        to = partner(k)
        pltpu.make_async_remote_copy(
            ret_out.at[to], ret_in.at[me], ret_send, ret_recv, device_id={"wave": to}, device_id_type=MESH
        ).start()
        return c

    lax.fori_loop(0, n - 1, send_back, 0)
    ret_in[me] = ret_out[me]

    def wait_level(k, acc):
        level_copy(k, lev).wait_recv()
        return acc + level_in[k]

    deeper = lax.fori_loop(lev + 1, depth, wait_level, jnp.zeros((4, span), F32))
    for slot in range(2):
        for part in range(2):
            at = slot * 2 + part
            below[slot, part] = below[slot, part] + deeper[at : at + 1]
    row_of = iota((128, 128), 0)
    picked_of = (row_of // 16 % 2) * 64 + (row_of // 4 % 4) * 8 + row_of % 4
    picked_of = picked_of + which_of(row_of // 32) * 32 + (row_of // 64) * 4
    pick = (iota((128, 128), 1) == picked_of).astype(BF16)

    pltpu.make_async_copy(ret_in.at[others], ret_in.at[others], ret_recv).wait()
    stage[...] = ret_in[...].reshape(n * ROWS, 128).astype(F32)
    for slot in range(2):
        rows_in = [stage[pl.ds(slot * quads + b, n, stride=ROWS), :] for b in range(quads)]
        rows_in = jnp.concatenate(rows_in, axis=0).astype(BF16)
        left = lax.dot_general(pick, rows_in, NT, preferred_element_type=F32).astype(BF16)
        zero = jnp.zeros((4, span), F32)
        acc = jnp.concatenate([zero, zero, below[slot, 0], zero, zero, zero, below[slot, 1], zero], axis=0)
        for k in range(4):
            acc = acc + jnp.dot(left[k * 32 : k * 32 + 32], block(slot, k), preferred_element_type=F32)
        live = column < span - waves[slot]
        out_ref[slot] = jnp.where(live, acc, 0.0).astype(BF16)

    pltpu.make_async_copy(wave_rows.at[others], wave_rows.at[others], wave_send).wait()
    pltpu.make_async_copy(msg_out.at[others], msg_out.at[others], out_send).wait()
    pltpu.make_async_copy(ret_out.at[others], ret_out.at[others], ret_send).wait()

    def sent_level(k, c):
        level_copy(lev, k).wait_send()
        return c

    lax.fori_loop(0, lev, sent_level, 0)


def solution(mesh):
    plan = Plan(mesh)
    n, depth, span, lat = plan.groups, plan.depth, plan.span, plan.lat
    dma = pltpu.SemaphoreType.DMA

    def body(spec, legendre, layer_depth_share, quad_weight, wave_of_slot):
        any_spec = pl.BlockSpec(memory_space=pltpu.HBM)
        return pl.pallas_call(
            functools.partial(kernel, plan),
            out_shape=jax.ShapeDtypeStruct((2, 32, span), BF16),
            in_specs=[any_spec] * 5,
            out_specs=pl.BlockSpec(memory_space=pltpu.VMEM),
            scratch_shapes=[
                pltpu.VMEM((2, 32, span), BF16),
                pltpu.VMEM((2, lat, span), BF16),
                pltpu.VMEM((2, 2, lat // 4, span), BF16),
                pltpu.SMEM((4,), F32),
                pltpu.SMEM((lat,), F32),
                pltpu.SMEM((2,), jnp.int32),
                pltpu.VMEM((1, 128), F32),
                pltpu.VMEM((n, 1, 128), F32),
                pltpu.VMEM((n * ROWS, 128), F32),
                pltpu.VMEM((n, ROWS, 128), BF16),
                pltpu.VMEM((n, ROWS, 128), BF16),
                pltpu.VMEM((n, ROWS, 128), BF16),
                pltpu.VMEM((n, ROWS, 128), BF16),
                pltpu.VMEM((2 * plan.quads, 128, 256), BF16),
                pltpu.VMEM((2 * plan.quads, 2, LOW + plan.coarse, 128), F32),
                pltpu.VMEM((plan.table_rows, 256), BF16),
                pltpu.VMEM((4, span), F32),
                pltpu.VMEM((depth, 4, span), F32),
                pltpu.VMEM((2, 2, 4, span), F32),
                dma((6,)), dma, dma, dma, dma, dma, dma, dma((depth,)), dma((depth,)),
            ],
            compiler_params=pltpu.CompilerParams(
                collective_id=0, has_side_effects=True, vmem_limit_bytes=63 * 1024 * 1024
            ),
        )(spec, legendre, layer_depth_share, quad_weight, wave_of_slot)

    in_specs = (P("wave", "lev", None), P("wave", None, None), P("lev"), P(), P("wave"))
    return jax.shard_map(body, mesh=mesh, in_specs=in_specs, out_specs=P("wave", "lev", None), check_vma=False)
```

time: 44.4 us -> 39.6 us (0.89)
  Pallas kernels: 42.7 us -> 37.9 us
    pallas_call x1, Pallas kernels: 42.7 us -> 37.9 us  [body(): pl.pallas_call(functools.partial(kernel, plan), out_shape=jax.ShapeDtypeS...]
where the time goes in v2:
time: 39.6 us; the launch traced here: 39.5 us
  Pallas kernels  37.9 us (96%)
  local copies, waits for them, and re-layouts  1.53 us (4%)
    pallas_call x1, Pallas kernels, body(): pl.pallas_call(functools.partial(kernel, plan), out_shape=jax.ShapeDtypeS...  37.9 us
    unnamed x1, local copies, waits for them, and re-layouts  1.53 us

profile of v2, /device:TPU:1, one launch (start us, length us, event | category | flops | bytes accessed | tf_op | source)
XLA Modules:
  0.0 39.5 jit_solution(1817116880748322226)
XLA Ops:
  0.0 37.9 %shard_map.55 = bf16[2,32,640]{2,1,0:T(8,128)(2,1)} custom-call(bf16[2,32,640]{2,1,0:T(8,128)(2,1)} %spec_hbm.1, bf16[2,1280,640]{2,1,0:T(8,128)(2,1)} %leg_hbm.1, f32[4]{0:T(128)} %share_hbm.1, f32[1280]{0:T(1024)} %quad_hbm.1, s32[2]{0:T(128)} %wave_hbm.1), custom_call_target="tpu_custom_call" | custom-call | tf_op jit(solution)/shard_map/pallas_call | solution.py:325
  37.9 1.5 %copy.7 = bf16[2,32,640]{2,1,0:T(8,128)(2,1)} copy(bf16[2,32,640]{2,1,0:T(8,128)(2,1)} %shard_map.55) | data formatting | bytes 163840

commit v3 on v2

--- a/solution.py
+++ b/solution.py
@@ -11,7 +11,6 @@
 MESH = pl.DeviceIdType.MESH
 F32 = jnp.float32
 BF16 = jnp.bfloat16
-ROWS = 16
 LOW = 32
 NT = (((1,), (1,)), ((), ()))
 
@@ -45,6 +44,7 @@
         self.span = 640
         self.quarter = self.lat // 4
         self.quads = self.quarter // self.groups
+        self.rows = 2 * self.quads
         self.blocks = []
         first = 0
         for quad in range(self.quads):
@@ -70,10 +70,13 @@
     n, depth, quads, span = plan.groups, plan.depth, plan.quads, plan.span
     me = lax.axis_index("wave")
     lev = lax.axis_index("lev")
-    quarter = plan.quarter
+    quarter, rows = plan.quarter, plan.rows
 
     def partner(k):
         return lax.rem(me + n // 2 + (2 * (k % 2) - 1) * ((k + 1) // 2), n)
+
+    def message(ref, k):
+        return ref.at[pl.ds(pl.multiple_of(k * rows, 2), rows)]
 
     barrier = pltpu.get_barrier_semaphore()
 
@@ -133,7 +136,6 @@
             return leg_turned[slot, k // 2]
         return leg[slot, k * quarter : (k + 1) * quarter, :]
 
-    stage[...] = jnp.zeros_like(stage)
     for slot in range(2):
         loads[4 + slot].wait()
         for k in (1, 3):
@@ -147,8 +149,8 @@
             term = lax.dot_general(block(slot, k), weights, NT, preferred_element_type=F32)
             acc = term if acc is None else acc + term
         for b in range(quads):
-            stage[pl.ds(slot * quads + b, n, stride=ROWS), :] = acc[b * n : (b + 1) * n]
-    msg_out[...] = stage[...].astype(BF16).reshape(n, ROWS, 128)
+            stage[pl.ds(slot * quads + b, n, stride=rows), :] = acc[b * n : (b + 1) * n]
+    msg_out[...] = stage[...].astype(BF16)
 
     pl.semaphore_wait(barrier, n - 1 + lev)
 
@@ -164,7 +166,7 @@
     def send_out(k, c):
         to = partner(k)
         pltpu.make_async_remote_copy(
-            msg_out.at[to], msg_in.at[me], out_send, out_recv, device_id={"wave": to}, device_id_type=MESH
+            message(msg_out, to), message(msg_in, me), out_send, out_recv, device_id={"wave": to}, device_id_type=MESH
         ).start()
         return c
 
@@ -182,8 +184,8 @@
 
     lax.fori_loop(0, lev, send_level, 0)
     wave_rows[me] = wave_row[...]
-    msg_in[me] = msg_out[me]
-    others = pl.ds(0, n - 1)
+    pltpu.make_async_copy(message(msg_out, me), message(msg_in, me), out_recv).start()
+    others, most = pl.ds(0, n - 1), pl.ds(0, (n - 1) * rows)
     loads[3].wait()
     pltpu.make_async_copy(wave_rows.at[others], wave_rows.at[others], wave_recv).wait()
     m = jnp.sum(wave_rows[...], axis=0)
@@ -209,14 +211,14 @@
             table[to : to + LOW, 0:128] = (ch * cl - sh * sl).astype(BF16)
             table[to : to + LOW, 128:256] = (sh * cl + ch * sl).astype(BF16)
 
-    pltpu.make_async_copy(msg_in.at[others], msg_in.at[others], out_recv).wait()
-    stage[...] = msg_in[...].reshape(n * ROWS, 128).astype(F32)
+    pltpu.make_async_copy(msg_in, msg_in, out_recv).wait()
+    stage[...] = msg_in[...].astype(F32)
     double = jnp.where(m == 0.0, 1.0, 2.0)
     parity = 1.0 - 2.0 * (m - 2.0 * jnp.floor(m * 0.5))
     keep = [2.0 * m < length for _, _, length in lengths]
     none = jnp.zeros((32, 128), F32)
     for b in range(quads):
-        rows_in = [stage[pl.ds(slot * quads + b, n, stride=ROWS), :] for slot in range(2)]
+        rows_in = [stage[pl.ds(slot * quads + b, n, stride=rows), :] for slot in range(2)]
         turned = jnp.concatenate(rows_in, axis=0).T
         for which in range(2):
             amplitude = jnp.where(keep[2 * b + which], double, 0.0)
@@ -264,18 +266,18 @@
             sums.append((jnp.where(keep[at], real * scale, 0.0), jnp.where(keep[at], imag * scale, 0.0)))
         merged = jnp.concatenate([sums[0][0], sums[1][0], sums[0][1], sums[1][1]], axis=0).T
         for slot in range(2):
-            stage[pl.ds(slot * quads + b, n, stride=ROWS), :] = merged[slot * n : (slot + 1) * n]
-    ret_out[...] = stage[...].astype(BF16).reshape(n, ROWS, 128)
+            stage[pl.ds(slot * quads + b, n, stride=rows), :] = merged[slot * n : (slot + 1) * n]
+    ret_out[...] = stage[...].astype(BF16)
 
     def send_back(k, c):
         to = partner(k)
         pltpu.make_async_remote_copy(
-            ret_out.at[to], ret_in.at[me], ret_send, ret_recv, device_id={"wave": to}, device_id_type=MESH
+            message(ret_out, to), message(ret_in, me), ret_send, ret_recv, device_id={"wave": to}, device_id_type=MESH
         ).start()
         return c
 
     lax.fori_loop(0, n - 1, send_back, 0)
-    ret_in[me] = ret_out[me]
+    pltpu.make_async_copy(message(ret_out, me), message(ret_in, me), ret_recv).start()
 
     def wait_level(k, acc):
         level_copy(k, lev).wait_recv()
@@ -291,10 +293,10 @@
     picked_of = picked_of + which_of(row_of // 32) * 32 + (row_of // 64) * 4
     pick = (iota((128, 128), 1) == picked_of).astype(BF16)
 
-    pltpu.make_async_copy(ret_in.at[others], ret_in.at[others], ret_recv).wait()
-    stage[...] = ret_in[...].reshape(n * ROWS, 128).astype(F32)
+    pltpu.make_async_copy(ret_in, ret_in, ret_recv).wait()
+    stage[...] = ret_in[...].astype(F32)
     for slot in range(2):
-        rows_in = [stage[pl.ds(slot * quads + b, n, stride=ROWS), :] for b in range(quads)]
+        rows_in = [stage[pl.ds(slot * quads + b, n, stride=rows), :] for b in range(quads)]
         rows_in = jnp.concatenate(rows_in, axis=0).astype(BF16)
         left = lax.dot_general(pick, rows_in, NT, preferred_element_type=F32).astype(BF16)
         zero = jnp.zeros((4, span), F32)
@@ -305,8 +307,8 @@
         out_ref[slot] = jnp.where(live, acc, 0.0).astype(BF16)
 
     pltpu.make_async_copy(wave_rows.at[others], wave_rows.at[others], wave_send).wait()
-    pltpu.make_async_copy(msg_out.at[others], msg_out.at[others], out_send).wait()
-    pltpu.make_async_copy(ret_out.at[others], ret_out.at[others], ret_send).wait()
+    pltpu.make_async_copy(msg_out.at[most], msg_out.at[most], out_send).wait()
+    pltpu.make_async_copy(ret_out.at[most], ret_out.at[most], ret_send).wait()
 
     def sent_level(k, c):
         level_copy(lev, k).wait_send()
@@ -320,7 +322,7 @@
     n, depth, span, lat = plan.groups, plan.depth, plan.span, plan.lat
     dma = pltpu.SemaphoreType.DMA
 
-    def body(spec, legendre, layer_depth_share, quad_weight, wave_of_slot):
+    def body(*args):
         any_spec = pl.BlockSpec(memory_space=pltpu.HBM)
         return pl.pallas_call(
             functools.partial(kernel, plan),
@@ -336,11 +338,11 @@
                 pltpu.SMEM((2,), jnp.int32),
                 pltpu.VMEM((1, 128), F32),
                 pltpu.VMEM((n, 1, 128), F32),
-                pltpu.VMEM((n * ROWS, 128), F32),
-                pltpu.VMEM((n, ROWS, 128), BF16),
-                pltpu.VMEM((n, ROWS, 128), BF16),
-                pltpu.VMEM((n, ROWS, 128), BF16),
-                pltpu.VMEM((n, ROWS, 128), BF16),
+                pltpu.VMEM((n * plan.rows, 128), F32),
+                pltpu.VMEM((n * plan.rows, 128), BF16),
+                pltpu.VMEM((n * plan.rows, 128), BF16),
+                pltpu.VMEM((n * plan.rows, 128), BF16),
+                pltpu.VMEM((n * plan.rows, 128), BF16),
                 pltpu.VMEM((2 * plan.quads, 128, 256), BF16),
                 pltpu.VMEM((2 * plan.quads, 2, LOW + plan.coarse, 128), F32),
                 pltpu.VMEM((plan.table_rows, 256), BF16),
@@ -350,9 +352,9 @@
                 dma((6,)), dma, dma, dma, dma, dma, dma, dma((depth,)), dma((depth,)),
             ],
             compiler_params=pltpu.CompilerParams(
-                collective_id=0, has_side_effects=True, vmem_limit_bytes=63 * 1024 * 1024
+                collective_id=0, has_side_effects=True, vmem_limit_bytes=24 * 1024 * 1024
             ),
-        )(spec, legendre, layer_depth_share, quad_weight, wave_of_slot)
+        )(*[pltpu.with_memory_space_constraint(x, pltpu.HBM) for x in args])
 
     in_specs = (P("wave", "lev", None), P("wave", None, None), P("lev"), P(), P("wave"))
     return jax.shard_map(body, mesh=mesh, in_specs=in_specs, out_specs=P("wave", "lev", None), check_vma=False)

time: 39.6 us -> 35.7 us (0.902)
  Pallas kernels: 37.9 us -> 35 us
  local copies, waits for them, and re-layouts: 1.53 us -> 0.64 us
    pallas_call x1, Pallas kernels: 37.9 us -> 35 us  [body(): pl.pallas_call(functools.partial(kernel, plan), out_shape=jax.ShapeDtypeS...]
    unnamed x1, local copies, waits for them, and re-layouts: 1.53 us -> 0.64 us
where the time goes in v3:
time: 35.7 us; the launch traced here: 35.6 us
  Pallas kernels  35 us (98%)
  local copies, waits for them, and re-layouts  0.64 us (2%)
    pallas_call x1, Pallas kernels, body(): pl.pallas_call(functools.partial(kernel, plan), out_shape=jax.ShapeDtypeS...  35 us

profile of v3, /device:TPU:1, one launch (start us, length us, event | category | flops | bytes accessed | tf_op | source)
XLA Modules:
  0.0 35.6 jit_solution(10003678615441083906)
XLA Ops:
  0.0 35.0 %shard_map.55 = bf16[2,32,640]{2,1,0:T(8,128)(2,1)S(1)} custom-call(bf16[2,32,640]{2,1,0:T(8,128)(2,1)} %spec_hbm.1, bf16[2,1280,640]{2,1,0:T(8,128)(2,1)} %leg_hbm.1, f32[4]{0:T(128)} %share_hbm.1, f32[1280]{0:T(1024)} %quad_hbm.1, s32[2]{0:T(128)} %wave_hbm.1), custom_call_target="tpu_custom_call" | custom-call | tf_op jit(solution)/shard_map/pallas_call | solution.py:327
  35.0 0.6 %copy.7 = bf16[2,32,640]{2,1,0:T(8,128)(2,1)} copy(bf16[2,32,640]{2,1,0:T(8,128)(2,1)S(1)} %shard_map.55) | data formatting | bytes 163840

commit v4 on v3

--- a/solution.py
+++ b/solution.py
@@ -72,25 +72,27 @@
     lev = lax.axis_index("lev")
     quarter, rows = plan.quarter, plan.rows
 
-    def partner(k):
-        return lax.rem(me + n // 2 + (2 * (k % 2) - 1) * ((k + 1) // 2), n)
+    def partners(visit):
+        def at(offset):
+            to = me + offset
+            visit(jnp.where(to >= n, to - n, to))
+
+        def both(p):
+            at(n // 2 - p)
+            at(n // 2 + p)
+
+        def several(i, c):
+            for u in range(3):
+                both(3 * i + u + 1)
+            return c
+
+        at(n // 2)
+        lax.fori_loop(0, (n // 2 - 1) // 3, several, 0)
+        for p in range((n // 2 - 1) // 3 * 3 + 1, n // 2):
+            both(p)
 
     def message(ref, k):
         return ref.at[pl.ds(pl.multiple_of(k * rows, 2), rows)]
-
-    barrier = pltpu.get_barrier_semaphore()
-
-    def greet(k, c):
-        pl.semaphore_signal(barrier, inc=1, device_id={"wave": partner(k)}, device_id_type=MESH)
-        return c
-
-    lax.fori_loop(0, n - 1, greet, 0)
-
-    def greet_level(k, c):
-        pl.semaphore_signal(barrier, inc=1, device_id={"lev": k}, device_id_type=MESH)
-        return c
-
-    lax.fori_loop(lev + 1, depth, greet_level, 0)
 
     loads = [
         pltpu.make_async_copy(wave_hbm, waves, load_sem.at[0]),
@@ -102,6 +104,20 @@
     ]
     for load in loads:
         load.start()
+
+    barrier = pltpu.get_barrier_semaphore()
+
+    def greet(to):
+        pl.semaphore_signal(barrier, inc=1, device_id={"wave": to}, device_id_type=MESH)
+
+    partners(greet)
+
+    def greet_level(k, c):
+        pl.semaphore_signal(barrier, inc=1, device_id={"lev": k}, device_id_type=MESH)
+        return c
+
+    lax.fori_loop(lev + 1, depth, greet_level, 0)
+
     loads[0].wait()
     lane = iota((1, 128), 1)
     row = jnp.where(lane == me, waves[0], 0) + jnp.where(lane == me + n, waves[1], 0)
@@ -154,23 +170,19 @@
 
     pl.semaphore_wait(barrier, n - 1 + lev)
 
-    def send_wave(k, c):
+    def send_wave(to):
         pltpu.make_async_remote_copy(
-            wave_row, wave_rows.at[me], wave_send, wave_recv,
-            device_id={"wave": partner(k)}, device_id_type=MESH,
+            wave_row, wave_rows.at[pl.ds(me, 1)], wave_send, wave_recv, device_id={"wave": to}, device_id_type=MESH
         ).start()
-        return c
-
-    lax.fori_loop(0, n - 1, send_wave, 0)
-
-    def send_out(k, c):
-        to = partner(k)
+
+    partners(send_wave)
+
+    def send_out(to):
         pltpu.make_async_remote_copy(
             message(msg_out, to), message(msg_in, me), out_send, out_recv, device_id={"wave": to}, device_id_type=MESH
         ).start()
-        return c
-
-    lax.fori_loop(0, n - 1, send_out, 0)
+
+    partners(send_out)
 
     def level_copy(source, to):
         return pltpu.make_async_remote_copy(
@@ -183,12 +195,12 @@
         return c
 
     lax.fori_loop(0, lev, send_level, 0)
-    wave_rows[me] = wave_row[...]
+    pltpu.make_async_copy(wave_row, wave_rows.at[pl.ds(me, 1)], wave_recv).start()
     pltpu.make_async_copy(message(msg_out, me), message(msg_in, me), out_recv).start()
     others, most = pl.ds(0, n - 1), pl.ds(0, (n - 1) * rows)
     loads[3].wait()
-    pltpu.make_async_copy(wave_rows.at[others], wave_rows.at[others], wave_recv).wait()
-    m = jnp.sum(wave_rows[...], axis=0)
+    pltpu.make_async_copy(wave_rows, wave_rows, wave_recv).wait()
+    m = jnp.sum(wave_rows[...], axis=0, keepdims=True)
 
     index = iota((LOW + plan.coarse, 1), 0)
     step = jnp.where(index < LOW, index, (index - LOW) * LOW).astype(F32)
@@ -269,14 +281,12 @@
             stage[pl.ds(slot * quads + b, n, stride=rows), :] = merged[slot * n : (slot + 1) * n]
     ret_out[...] = stage[...].astype(BF16)
 
-    def send_back(k, c):
-        to = partner(k)
+    def send_back(to):
         pltpu.make_async_remote_copy(
             message(ret_out, to), message(ret_in, me), ret_send, ret_recv, device_id={"wave": to}, device_id_type=MESH
         ).start()
-        return c
-
-    lax.fori_loop(0, n - 1, send_back, 0)
+
+    partners(send_back)
     pltpu.make_async_copy(message(ret_out, me), message(ret_in, me), ret_recv).start()
 
     def wait_level(k, acc):
@@ -337,7 +347,7 @@
                 pltpu.SMEM((lat,), F32),
                 pltpu.SMEM((2,), jnp.int32),
                 pltpu.VMEM((1, 128), F32),
-                pltpu.VMEM((n, 1, 128), F32),
+                pltpu.VMEM((n, 128), F32),
                 pltpu.VMEM((n * plan.rows, 128), F32),
                 pltpu.VMEM((n * plan.rows, 128), BF16),
                 pltpu.VMEM((n * plan.rows, 128), BF16),

time: 35.7 us -> 33.3 us (0.933)
  Pallas kernels: 35 us -> 32.5 us
    pallas_call x1, Pallas kernels: 35 us -> 32.5 us  [body(): pl.pallas_call(functools.partial(kernel, plan), out_shape=jax.ShapeDtypeS...]
where the time goes in v4:
time: 33.3 us; the launch traced here: 33.2 us
  Pallas kernels  32.5 us (98%)
  local copies, waits for them, and re-layouts  0.64 us (2%)
    pallas_call x1, Pallas kernels, body(): pl.pallas_call(functools.partial(kernel, plan), out_shape=jax.ShapeDtypeS...  32.5 us

profile of v4, /device:TPU:1, one launch (start us, length us, event | category | flops | bytes accessed | tf_op | source)
XLA Modules:
  0.0 33.2 jit_solution(7134198431621425258)
XLA Ops:
  0.0 32.5 %shard_map.55 = bf16[2,32,640]{2,1,0:T(8,128)(2,1)S(1)} custom-call(bf16[2,32,640]{2,1,0:T(8,128)(2,1)} %spec_hbm.1, bf16[2,1280,640]{2,1,0:T(8,128)(2,1)} %leg_hbm.1, f32[4]{0:T(128)} %share_hbm.1, f32[1280]{0:T(1024)} %quad_hbm.1, s32[2]{0:T(128)} %wave_hbm.1), custom_call_target="tpu_custom_call" | custom-call | tf_op jit(solution)/shard_map/pallas_call | solution.py:337
  32.5 0.6 %copy.7 = bf16[2,32,640]{2,1,0:T(8,128)(2,1)} copy(bf16[2,32,640]{2,1,0:T(8,128)(2,1)S(1)} %shard_map.55) | data formatting | bytes 163840

commit v5 on v4

--- a/solution.py
+++ b/solution.py
@@ -12,6 +12,7 @@
 F32 = jnp.float32
 BF16 = jnp.bfloat16
 LOW = 32
+AHEAD = 5
 NT = (((1,), (1,)), ((), ()))
 
 
@@ -56,16 +57,16 @@
                 self.blocks.append((quad, which, points, first))
                 first += points
         self.table_rows = first
-        self.coarse = round_up(max(b[2] for b in self.blocks) // LOW, 8)
+        self.coarse = round_up(max(b[2] for b in self.blocks), 8 * LOW) // LOW
 
 
 def kernel(
     plan,
     spec_hbm, leg_hbm, share_hbm, quad_hbm, wave_hbm, out_ref,
     spec, leg, leg_turned, share, quad, waves,
-    wave_row, wave_rows, stage, msg_out, msg_in, ret_out, ret_in,
+    wave_row, wave_rows, wave_all, stage, stage_out, msg_out, msg_in, ret_out, ret_in,
     coefs, base, table, level_out, level_in, below,
-    load_sem, wave_send, wave_recv, out_send, out_recv, ret_send, ret_recv, lev_send, lev_recv,
+    load_sem, wave_send, wave_recv, pass_send, pass_recv, out_send, out_recv, ret_send, ret_recv, lev_send, lev_recv,
 ):
     n, depth, quads, span = plan.groups, plan.depth, plan.quads, plan.span
     me = lax.axis_index("wave")
@@ -175,7 +176,10 @@
             wave_row, wave_rows.at[pl.ds(me, 1)], wave_send, wave_recv, device_id={"wave": to}, device_id_type=MESH
         ).start()
 
-    partners(send_wave)
+    @pl.when(lev > 0)
+    def _():
+        partners(send_wave)
+        pltpu.make_async_copy(wave_row, wave_rows.at[pl.ds(me, 1)], wave_recv).start()
 
     def send_out(to):
         pltpu.make_async_remote_copy(
@@ -195,41 +199,69 @@
         return c
 
     lax.fori_loop(0, lev, send_level, 0)
-    pltpu.make_async_copy(wave_row, wave_rows.at[pl.ds(me, 1)], wave_recv).start()
     pltpu.make_async_copy(message(msg_out, me), message(msg_in, me), out_recv).start()
     others, most = pl.ds(0, n - 1), pl.ds(0, (n - 1) * rows)
     loads[3].wait()
-    pltpu.make_async_copy(wave_rows, wave_rows, wave_recv).wait()
-    m = jnp.sum(wave_rows[...], axis=0, keepdims=True)
-
-    index = iota((LOW + plan.coarse, 1), 0)
-    step = jnp.where(index < LOW, index, (index - LOW) * LOW).astype(F32)
+
+    pass_on = pltpu.make_async_remote_copy(
+        wave_all, wave_all, pass_send, pass_recv, device_id={"lev": 0}, device_id_type=MESH
+    )
+
+    @pl.when(lev > 0)
+    def _():
+        pltpu.make_async_copy(wave_rows, wave_rows, wave_recv).wait()
+        wave_all[...] = jnp.sum(wave_rows[...], axis=0, keepdims=True)
+
+    @pl.when(lev == 1)
+    def _():
+        pass_on.start()
+
+    @pl.when(lev == 0)
+    def _():
+        pass_on.wait_recv()
+
+    m = wave_all[...]
+
+    index = iota((24, 1), 0)
+    step = jnp.where(index < 8, index, jnp.where(index < 12, (index - 8) * 8, (index - 12) * 256))
+    step = jnp.where(index < 16, step, (index - 16) * LOW).astype(F32)
     turns = step * m
-    lengths = []
-    for at, (b, which, points, first) in enumerate(plan.blocks):
-        q = me + b * n
-        if which == 1:
-            q = plan.lat // 2 - 1 - q
-        quart = (5 + q).astype(F32)
-        lengths.append((q, quart, quart * 4.0))
-        c, s = cos_sin(turns, quart, quart * 4.0)
-        base[at, 0] = c
-        base[at, 1] = s
-    for at, (b, which, points, first) in enumerate(plan.blocks):
-        cl, sl = base[at, 0, 0:LOW, :], base[at, 1, 0:LOW, :]
-        for a in range(points // LOW):
-            ch, sh = base[at, 0, LOW + a : LOW + a + 1, :], base[at, 1, LOW + a : LOW + a + 1, :]
-            to = first + a * LOW
-            table[to : to + LOW, 0:128] = (ch * cl - sh * sl).astype(BF16)
-            table[to : to + LOW, 128:256] = (sh * cl + ch * sl).astype(BF16)
-
-    pltpu.make_async_copy(msg_in, msg_in, out_recv).wait()
-    stage[...] = msg_in[...].astype(F32)
+    lengths = {}
+    keep = {}
     double = jnp.where(m == 0.0, 1.0, 2.0)
     parity = 1.0 - 2.0 * (m - 2.0 * jnp.floor(m * 0.5))
-    keep = [2.0 * m < length for _, _, length in lengths]
+
+    def rotated(c, s, at, r):
+        ch, sh = base[at, 0, r : r + 1, :], base[at, 1, r : r + 1, :]
+        return ch * c - sh * s, sh * c + ch * s
+
+    def make_tables(b):
+        for which in range(2):
+            at = 2 * b + which
+            _, _, points, first = plan.blocks[at]
+            q = me + b * n
+            if which == 1:
+                q = plan.lat // 2 - 1 - q
+            quart = (5 + q).astype(F32)
+            lengths[at] = (q, quart, quart * 4.0)
+            keep[at] = 2.0 * m < quart * 4.0
+            c, s = cos_sin(turns, quart, quart * 4.0)
+            base[at, 0, 0:24], base[at, 1, 0:24] = c, s
+            fine = [(c[0:8], s[0:8])] + [rotated(c[0:8], s[0:8], at, 8 + r) for r in range(1, 4)]
+            cl = jnp.concatenate([f[0] for f in fine], axis=0)
+            sl = jnp.concatenate([f[1] for f in fine], axis=0)
+            for r in range(1, round_up(points, 256) // 256):
+                high = rotated(c[16:24], s[16:24], at, 12 + r)
+                base[at, 0, 16 + 8 * r : 24 + 8 * r], base[at, 1, 16 + 8 * r : 24 + 8 * r] = high
+            for a in range(points // LOW):
+                to = first + a * LOW
+                ct, st = rotated(cl, sl, at, 16 + a)
+                table[to : to + LOW, 0:128] = ct.astype(BF16)
+                table[to : to + LOW, 128:256] = st.astype(BF16)
+
     none = jnp.zeros((32, 128), F32)
-    for b in range(quads):
+
+    def make_coefs(b):
         rows_in = [stage[pl.ds(slot * quads + b, n, stride=rows), :] for slot in range(2)]
         turned = jnp.concatenate(rows_in, axis=0).T
         for which in range(2):
@@ -240,8 +272,18 @@
             right = jnp.concatenate([none, imag, none, imag * -parity], axis=0)
             coefs[2 * b + which] = jnp.concatenate([left, right], axis=1).astype(BF16)
 
+    for b in range(AHEAD):
+        make_tables(b)
+    pltpu.make_async_copy(msg_in, msg_in, out_recv).wait()
+    stage[...] = msg_in[...].astype(F32)
+    for b in range(AHEAD):
+        make_coefs(b)
+
     sub = iota((8, 1), 0)
     for b in range(quads):
+        if b + AHEAD < quads:
+            make_tables(b + AHEAD)
+            make_coefs(b + AHEAD)
         sums = []
         for which in range(2):
             at = 2 * b + which
@@ -278,8 +320,8 @@
             sums.append((jnp.where(keep[at], real * scale, 0.0), jnp.where(keep[at], imag * scale, 0.0)))
         merged = jnp.concatenate([sums[0][0], sums[1][0], sums[0][1], sums[1][1]], axis=0).T
         for slot in range(2):
-            stage[pl.ds(slot * quads + b, n, stride=rows), :] = merged[slot * n : (slot + 1) * n]
-    ret_out[...] = stage[...].astype(BF16)
+            stage_out[pl.ds(slot * quads + b, n, stride=rows), :] = merged[slot * n : (slot + 1) * n]
+    ret_out[...] = stage_out[...].astype(BF16)
 
     def send_back(to):
         pltpu.make_async_remote_copy(
@@ -316,7 +358,14 @@
         live = column < span - waves[slot]
         out_ref[slot] = jnp.where(live, acc, 0.0).astype(BF16)
 
-    pltpu.make_async_copy(wave_rows.at[others], wave_rows.at[others], wave_send).wait()
+    @pl.when(lev > 0)
+    def _():
+        pltpu.make_async_copy(wave_rows.at[others], wave_rows.at[others], wave_send).wait()
+
+    @pl.when(lev == 1)
+    def _():
+        pass_on.wait_send()
+
     pltpu.make_async_copy(msg_out.at[most], msg_out.at[most], out_send).wait()
     pltpu.make_async_copy(ret_out.at[most], ret_out.at[most], ret_send).wait()
 
@@ -348,18 +397,20 @@
                 pltpu.SMEM((2,), jnp.int32),
                 pltpu.VMEM((1, 128), F32),
                 pltpu.VMEM((n, 128), F32),
+                pltpu.VMEM((1, 128), F32),
+                pltpu.VMEM((n * plan.rows, 128), F32),
                 pltpu.VMEM((n * plan.rows, 128), F32),
                 pltpu.VMEM((n * plan.rows, 128), BF16),
                 pltpu.VMEM((n * plan.rows, 128), BF16),
                 pltpu.VMEM((n * plan.rows, 128), BF16),
                 pltpu.VMEM((n * plan.rows, 128), BF16),
                 pltpu.VMEM((2 * plan.quads, 128, 256), BF16),
-                pltpu.VMEM((2 * plan.quads, 2, LOW + plan.coarse, 128), F32),
+                pltpu.VMEM((2 * plan.quads, 2, 16 + plan.coarse, 128), F32),
                 pltpu.VMEM((plan.table_rows, 256), BF16),
                 pltpu.VMEM((4, span), F32),
                 pltpu.VMEM((depth, 4, span), F32),
                 pltpu.VMEM((2, 2, 4, span), F32),
-                dma((6,)), dma, dma, dma, dma, dma, dma, dma((depth,)), dma((depth,)),
+                dma((6,)), dma, dma, dma, dma, dma, dma, dma, dma, dma((depth,)), dma((depth,)),
             ],
             compiler_params=pltpu.CompilerParams(
                 collective_id=0, has_side_effects=True, vmem_limit_bytes=24 * 1024 * 1024

time: 33.3 us -> 32.9 us (0.988)
  Pallas kernels: 32.5 us -> 32.1 us
    pallas_call x1, Pallas kernels: 32.5 us -> 32.1 us  [body(): pl.pallas_call(functools.partial(kernel, plan), out_shape=jax.ShapeDtypeS...]
where the time goes in v5:
time: 32.9 us; the launch traced here: 32.7 us
  Pallas kernels  32.1 us (98%)
  local copies, waits for them, and re-layouts  0.64 us (2%)
    pallas_call x1, Pallas kernels, body(): pl.pallas_call(functools.partial(kernel, plan), out_shape=jax.ShapeDtypeS...  32.1 us

profile of v5, /device:TPU:1, one launch (start us, length us, event | category | flops | bytes accessed | tf_op | source)
XLA Modules:
  0.0 32.7 jit_solution(8727267867815181346)
XLA Ops:
  0.0 32.1 %shard_map.55 = bf16[2,32,640]{2,1,0:T(8,128)(2,1)S(1)} custom-call(bf16[2,32,640]{2,1,0:T(8,128)(2,1)} %spec_hbm.1, bf16[2,1280,640]{2,1,0:T(8,128)(2,1)} %leg_hbm.1, f32[4]{0:T(128)} %share_hbm.1, f32[1280]{0:T(1024)} %quad_hbm.1, s32[2]{0:T(128)} %wave_hbm.1), custom_call_target="tpu_custom_call" | custom-call | tf_op jit(solution)/shard_map/pallas_call | solution.py:386
  32.1 0.6 %copy.7 = bf16[2,32,640]{2,1,0:T(8,128)(2,1)} copy(bf16[2,32,640]{2,1,0:T(8,128)(2,1)S(1)} %shard_map.55) | data formatting | bytes 163840
